TPU v7x, 16 devices: a 4x2x1 block of a 4x4x8 slice. The times are simulated.
16 devices in a mesh: dp: 4 (over y, z, core), tp: 4 (over x).
Axes of the slice: x: 4, y: 2, z: 1, core: 2. Of those that a mesh axis runs over, the one named last changes fastest.
The devices are a block of a 4x4x8 slice.
Arguments:
- x: bfloat16 [5632, 3072], P(('dp', 'tp')), parts along dimension 0
- dy: bfloat16 [5632, 3072], P(('dp', 'tp')), parts along dimension 0
- pre: bfloat16 [5632, 9216], P('dp', 'tp'), parts along dimension 0
- w_in: bfloat16 [3072, 9216], P(None, 'tp')
- w_down: bfloat16 [9216, 3072], P('tp')
Outputs:
- output 1: bfloat16 [5632, 3072], P(('dp', 'tp')), parts along dimension 0
- output 2: bfloat16 [12288, 9216], P('dp', 'tp'), parts along dimension 0
- output 3: bfloat16 [36864, 3072], P(('dp', 'tp')), parts along dimension 0
There are 4 independent parts. A program takes and returns all parts, laid end to end along the dimension named above; an argument that names none is the same for every part.
All inputs are finite; a program needn't handle non-finite values.
Results may differ from a plain program's by a relative error of at most 0.012.
Values are sent between devices in bfloat16 or wider.
A program may use at most 768 MiB of HBM per device.

v0:
```python
import jax
import jax.numpy as jnp


def act(pre):
    return jnp.square(jax.nn.relu(pre))


def solution(mesh):
    def step(x, dy, pre, w_in, w_down):
        hidden, back = jax.vjp(act, pre.astype(jnp.float32))
        d_hidden = jnp.dot(dy, w_down.T, preferred_element_type=jnp.float32)
        d_pre = back(d_hidden)[0].astype(jnp.bfloat16)
        dx = jnp.dot(d_pre, w_in.T)
        groups = mesh.shape["dp"]

        def by_group(a, b):
            a, b = (t.reshape(groups, -1, t.shape[-1]) for t in (a, b))
            product = jnp.einsum("gta,gtb->gab", a, b, preferred_element_type=jnp.float32)
            return product.astype(jnp.bfloat16).reshape(-1, b.shape[-1])

        return dx, by_group(x, d_pre), by_group(hidden.astype(jnp.bfloat16), dy)

    return step
```

profile of v0, /device:TPU:112, one launch (start us, length us, event | category | flops | bytes accessed | tf_op | source)
XLA Modules:
  0.0 266.9 jit_solution(17336826316054309372)
XLA Ops:
  7.2 0.1 all-gather.10.cloned.1.call-start
  7.2 0.7 all-gather.10.cloned.1.call-update
  8.0 0.1 all-gather.12.cloned.1.call-start
  8.0 0.7 all-gather.12.cloned.1.call-update
  8.8 0.1 reduce-scatter.4.cloned.1.call-start
  8.8 85.1 %all-gather.10.cloned.1.call-done = bf16[1408,3072]{1,0:T(8,128)(2,1)} async-done(((bf16[352,3072]{1,0:T(8,128)(2,1)}), bf16[1408,3072]{1,0:T(8,128)(2,1)}) %all-gather.10.cloned.1.call-update) | async-done | bytes 8650768 | tf_op args[1]
  93.9 27.9 %fusion.5 = bf16[1408,2304]{1,0:T(8,128)(2,1)S(1)} fusion(bf16[1408,2304]{1,0:T(8,128)(2,1)} %param, bf16[1408,3072]{1,0:T(8,128)(2,1)} %all-gather.10.cloned.1.call-done, bf16[2304,3072]{1,0:T(8,128)(2,1)} %param.2), kind=kOutput, calls=%fused_computation.10 | convolution fusion | flops 19954040832 | bytes 35782656 | tf_op jit(solution)/dot_general | solution.py:12
  121.9 0.0 copy-start
  121.9 2.8 %copy-done = bf16[1408,2304]{1,0:T(8,128)(2,1)} copy-done((bf16[1408,2304]{1,0:T(8,128)(2,1)}, bf16[1408,2304]{1,0:T(8,128)(2,1)S(1)}, u32[]{:S(2)}) %copy-start) | copy-done | bytes 6488088
  124.6 24.5 %fusion.9 = bf16[1408,3072]{1,0:T(8,128)(2,1)} fusion(bf16[1408,2304]{1,0:T(8,128)(2,1)S(1)} %fusion.5, bf16[3072,2304]{1,0:T(8,128)(2,1)} %param.3), kind=kOutput, calls=%fused_computation.13 | convolution fusion | flops 19931332608 | bytes 29294592 | tf_op jit(solution)/dot_general | solution.py:14
  149.1 0.1 reduce-scatter.4.cloned.1.call-update
  149.2 28.7 %all-gather.12.cloned.1.call-done = bf16[1408,3072]{1,0:T(8,128)(2,1)} async-done(((bf16[352,3072]{1,0:T(8,128)(2,1)}), bf16[1408,3072]{1,0:T(8,128)(2,1)}) %all-gather.12.cloned.1.call-update) | async-done | bytes 8650768 | tf_op jit(solution)/reshape | solution.py:18
  177.9 28.5 %fusion.3 = bf16[3072,2304]{0,1:T(8,128)(2,1)} fusion(bf16[1408,2304]{1,0:T(8,128)(2,1)} %copy-done, bf16[1408,3072]{1,0:T(8,128)(2,1)} %all-gather.12.cloned.1.call-done), kind=kOutput, calls=%fused_computation.8 | convolution fusion | flops 19938410496 | bytes 29294592 | tf_op jit(solution)/gta,gtb->gab/dot_general | solution.py:19
  206.4 18.6 %copy = bf16[3072,2304]{1,0:T(8,128)(2,1)} copy(bf16[3072,2304]{0,1:T(8,128)(2,1)} %fusion.3) | data formatting | bytes 28311552
  225.0 28.6 %convolution_convert_fusion = bf16[2304,3072]{1,0:T(8,128)(2,1)} fusion(bf16[1408,3072]{1,0:T(8,128)(2,1)} %all-gather.10.cloned.1.call-done, bf16[1408,2304]{1,0:T(8,128)(2,1)} %param), kind=kOutput, calls=%fused_computation | convolution fusion | flops 19951386624 | bytes 29294592 | tf_op jit(solution)/gta,gtb->gab/dot_general | solution.py:19
  253.6 6.8 %reduce-scatter.4.cloned.1.call-done = bf16[352,3072]{1,0:T(8,128)(2,1)} async-done(((bf16[1408,3072]{1,0:T(8,128)(2,1)}), bf16[352,3072]{1,0:T(8,128)(2,1)}) %reduce-scatter.4.cloned.1.call-update) | async-done | bytes 2162704
Async XLA Ops:
  7.2 86.7 %all-gather.10.cloned.1.call-start = ((), (), s32[]{:S(2)}) async-start(), calls=%async_computation.1 | async-start | bytes 10813440 | tf_op args[1]
  8.0 169.9 %all-gather.12.cloned.1.call-start = ((), (), s32[]{:S(2)}) async-start(), calls=%async_computation.2 | async-start | bytes 10813440 | tf_op jit(solution)/reshape | solution.py:18
  8.8 251.6 %reduce-scatter.4.cloned.1.call-start = ((), (), s32[]{:S(2)}) async-start(), calls=%async_computation.3 | async-start | bytes 10813440
  121.9 2.8 %copy-start = (bf16[1408,2304]{1,0:T(8,128)(2,1)}, bf16[1408,2304]{1,0:T(8,128)(2,1)S(1)}, u32[]{:S(2)}) copy-start(bf16[1408,2304]{1,0:T(8,128)(2,1)S(1)} %fusion.5) | copy-start | bytes 19464196
Sparse Core Ops, SparseCore 0:
  9.6 84.3 all-gather.9
  95.5 82.3 all-gather.11
  180.8 79.4 reduce-scatter.3
where the time goes:
time: 267 us
  waiting for transfers between devices  122 us (46%)
  matrix products  110 us (41%)
  local copies, waits for them, and re-layouts  21.4 us (8%)
  between operations  13.8 us (5%)
    unnamed x5, waiting for transfers between devices  93.3 us
    dot_general x2, matrix products, by_group(): jnp.einsum('gta,gtb->gab', a, b, preferred_element_type=jnp.float32)  57.1 us
    reshape x1, waiting for transfers between devices, by_group(): a, b = (t.reshape(groups, -1, t.shape[-1]) for t in (a, b))  28.7 us
    dot_general x1, matrix products, step(): d_hidden = jnp.dot(dy, w_down.T, preferred_element_type=jnp.float32)  27.9 us
    dot_general x1, matrix products, step(): dx = jnp.dot(d_pre, w_in.T)  24.5 us
    unnamed x3, local copies, waits for them, and re-layouts  21.4 us
  transfers between devices with their start and end apart: 3, of which 3 were waited for; matrix products, arithmetic and copies ran while one was open for 48% of the time, Pallas kernels for 0%

commit v1 on v0

v1 whole, which is shorter than its diff:
```python
import functools

import jax
import jax.numpy as jnp
from jax import lax
from jax.experimental import pallas as pl
from jax.experimental.pallas import tpu as pltpu
from jax.sharding import PartitionSpec as P

NT = (((1,), (1,)), ((), ()))
TN = (((0,), (0,)), ((), ()))
F32, BF16 = jnp.float32, jnp.bfloat16
TILE = 768
VMEM_LIMIT = 60 * 2**20


def act(pre):
    return jnp.square(jax.nn.relu(pre))


def backward_body(nd, pieces, blocks, chained, *refs):
    refs = refs[1 + chained:]
    dys, pres, (wd, wi), refs = refs[:pieces], refs[pieces:pieces + blocks], refs[pieces + blocks:pieces + blocks + 2], refs[pieces + blocks + 2:]
    dp_out, *t_out = refs[:2] if blocks == 1 else refs[:5]
    dp_all, *dy_all = refs[1 + len(t_out):]
    i = pl.program_id(0)
    rows = dp_out.shape[0] // blocks
    half = rows // 2
    tile = wd.shape[0]
    if pieces == 1:
        dy_all = dys[0]
    else:
        dy_all = dy_all[0]

        @pl.when(i == 0)
        def _():
            at = 0
            for dy in dys:
                dy_all[at:at + dy.shape[0]] = dy[...]
                at += dy.shape[0]

    @pl.when(i < nd)
    def _():
        d_hidden = lax.dot_general(dy_all[...], wd[...], NT, preferred_element_type=F32)
        for k in range(blocks):
            part = slice(k * rows, (k + 1) * rows)
            dp = (d_hidden[part] * (2.0 * jnp.maximum(pres[k][...].astype(F32), 0.0))).astype(BF16)
            dp_out[part] = dp
            dp_all[part, pl.ds(pl.multiple_of(i * tile, tile), tile)] = dp

    @pl.when(i >= nd)
    def _():
        t = lax.dot_general(dp_all[...], wi[...], NT, preferred_element_type=F32)
        if blocks == 1:
            t_out[0][...] = t
        else:
            first_a, first_b, rest_a, rest_b = t_out
            first_a[...] = t[:half].astype(BF16)
            rest_b[...] = t[half:rows]
            rest_a[...] = t[rows:rows + half]
            first_b[...] = t[rows + half:].astype(BF16)


def backward(dys, owners, pre, w_in, w_down, place, d_pre=None):
    chained = [] if d_pre is None else [d_pre]
    blocks = len(owners)
    total, d = sum(v.shape[0] for v in dys), dys[0].shape[1]
    rows, ff = total // blocks, pre.shape[1]
    half = rows // 2
    nd, ni = ff // TILE, d // TILE
    phase1 = lambda i: jnp.minimum(i, nd - 1)
    phase2 = lambda i: jnp.maximum(i - nd, 0)

    def pre_spec(k):
        return pl.BlockSpec((rows, TILE), lambda i, o: (o[k], phase1(i)))

    terms = [(rows, F32)] if blocks == 1 else [(half, BF16), (half, BF16), (half, F32), (half, F32)]
    return pl.pallas_call(
        functools.partial(backward_body, nd, len(dys), blocks, len(chained)),
        grid_spec=pltpu.PrefetchScalarGridSpec(
            num_scalar_prefetch=1,
            grid=(nd + ni,),
            in_specs=[pl.BlockSpec(memory_space=pl.ANY)] * len(chained)
            + [pl.BlockSpec(v.shape, lambda i, o: (0, 0)) for v in dys]
            + [pre_spec(k) for k in range(blocks)]
            + [pl.BlockSpec((TILE, d), lambda i, o: (phase1(i), 0)), pl.BlockSpec((TILE, ff), lambda i, o: (phase2(i), 0))],
            out_specs=[pl.BlockSpec((total, TILE), lambda i, o: (place, phase1(i)))]
            + [pl.BlockSpec((r, TILE), lambda i, o: (0, phase2(i))) for r, _ in terms],
            scratch_shapes=[pltpu.VMEM((total, ff), BF16)] + [pltpu.VMEM((total, d), BF16)] * (len(dys) > 1),
        ),
        out_shape=[jax.ShapeDtypeStruct((pre.shape[0], ff), BF16)] + [jax.ShapeDtypeStruct((r, d), t) for r, t in terms],
        input_output_aliases={1: 0} if chained else {},
        compiler_params=pltpu.CompilerParams(vmem_limit_bytes=VMEM_LIMIT, dimension_semantics=("arbitrary",)),
        cost_estimate=pl.CostEstimate(flops=4 * total * d * ff, bytes_accessed=4 * d * ff, transcendentals=0),
    )(jnp.stack(owners).astype(jnp.int32), *chained, *dys, *[pre] * blocks, w_down, w_in)


def dw_down_body(pieces, *refs):
    refs = refs[1:]
    pres, dys, (out, hidden, dy_all) = refs[:4], refs[4:4 + pieces], refs[4 + pieces:]

    @pl.when(pl.program_id(1) == 0)
    def _():
        at = 0
        for pre in pres:
            hidden[at:at + pre.shape[0]] = act(pre[...].astype(F32)).astype(BF16)
            at += pre.shape[0]

    at = 0
    for dy in dys:
        dy_all[at:at + dy.shape[0]] = dy[...]
        at += dy.shape[0]
    out[...] = lax.dot_general(hidden[...], dy_all[...], TN, preferred_element_type=F32).astype(BF16)


def grad_w_down(pre, owners, dys):
    rows, ff = pre.shape
    block, d = rows // len(owners), dys[0].shape[1]
    m, tn = ff // 2, TILE
    return pl.pallas_call(
        functools.partial(dw_down_body, len(dys)),
        grid_spec=pltpu.PrefetchScalarGridSpec(
            num_scalar_prefetch=1,
            grid=(ff // m, d // tn),
            in_specs=[pl.BlockSpec((block, m), functools.partial(lambda k, i, j, o: (o[k], i), k)) for k in range(len(owners))]
            + [pl.BlockSpec((v.shape[0], tn), lambda i, j, o: (0, j)) for v in dys],
            out_specs=pl.BlockSpec((m, tn), lambda i, j, o: (i, j)),
            scratch_shapes=[pltpu.VMEM((rows, m), BF16), pltpu.VMEM((rows, tn), BF16)],
        ),
        out_shape=jax.ShapeDtypeStruct((ff, d), BF16),
        compiler_params=pltpu.CompilerParams(vmem_limit_bytes=VMEM_LIMIT, dimension_semantics=("arbitrary", "arbitrary")),
        cost_estimate=pl.CostEstimate(flops=2 * rows * ff * d, bytes_accessed=2 * (rows * ff + 2 * rows * d + ff * d), transcendentals=0),
    )(jnp.stack(owners).astype(jnp.int32), *[pre] * len(owners), *dys)


def dw_in_body(columns, *refs):
    pieces = len(columns)
    xs, d_pre, (out, x_all, sems) = refs[:pieces], refs[pieces], refs[-3:]

    @pl.when(pl.program_id(0) == 0)
    def _():
        copies, at = [], 0
        for k, (x, c) in enumerate(zip(xs, columns)):
            src = x.at[:, pl.ds(c, x_all.shape[1])]
            copies.append(pltpu.make_async_copy(src, x_all.at[pl.ds(at, x.shape[0])], sems.at[k]))
            at += x.shape[0]
        for copy in copies:
            copy.start()
        for copy in copies:
            copy.wait()

    out[...] = lax.dot_general(x_all[...], d_pre[...], TN, preferred_element_type=F32).astype(BF16)


def grad_w_in(xs, d_pre, part, d, out=None):
    rows, ff = d_pre.shape
    m, tn = d // 2, TILE // 2
    columns = [part * m if x.shape[1] == d else 0 for x in xs]
    chained = [] if out is None else [out]
    return pl.pallas_call(
        functools.partial(dw_in_body, columns),
        grid=(ff // tn,),
        in_specs=[pl.BlockSpec(memory_space=pl.ANY)] * len(xs)
        + [pl.BlockSpec((rows, tn), lambda i: (0, i))]
        + [pl.BlockSpec(memory_space=pl.ANY)] * len(chained),
        out_specs=pl.BlockSpec((m, tn), lambda i: (part, i)),
        scratch_shapes=[pltpu.VMEM((rows, m), BF16), pltpu.SemaphoreType.DMA((len(xs),))],
        out_shape=jax.ShapeDtypeStruct((d, ff), BF16),
        input_output_aliases={len(xs) + 1: 0} if chained else {},
        compiler_params=pltpu.CompilerParams(vmem_limit_bytes=VMEM_LIMIT, dimension_semantics=("arbitrary",)),
        cost_estimate=pl.CostEstimate(flops=2 * rows * m * ff, bytes_accessed=2 * (rows * m + rows * ff + m * ff), transcendentals=0),
    )(*xs, d_pre, *chained)


def solution(mesh):
    n = mesh.shape["tp"]
    right = [(i, (i + 1) % n) for i in range(n)]
    left = [(i, (i - 1) % n) for i in range(n)]

    def send(a, b):
        a = lax.ppermute(a, "tp", right)
        b = lax.ppermute(b, "tp", left)
        return a, b

    def add(term, got):
        return (term + got.astype(F32)).astype(BF16)

    def step(x, dy, pre, w_in, w_down):
        me = lax.axis_index("tp")
        rows, d = x.shape
        half, m = rows // 2, d // 2
        lo, ro, own, oo = lax.rem(me + n - 1, n), lax.rem(me + 1, n), me, lax.rem(me + 2, n)

        dy_lo, dy_ro = send(dy, dy)
        top, bottom = x[:half], x[half:]
        x_lot, x_rob = send(top, bottom)
        d_pre, t0 = backward([dy], [own], pre, w_in, w_down, 2)
        dy_ot, dy_ob = send(dy_lo[:half], dy_ro[half:])
        d_pre, s, u, rest_a, rest_b = backward([dy_lo, dy_ro], [lo, ro], pre, w_in, w_down, 0, d_pre)
        s, u = send(s, u)
        x_lob, x_rot = send(bottom, top)
        x_ota, x_oba = send(x_lot[:, :m], x_rob[:, :m])
        d_pre, t3 = backward([dy_ot, dy_ob], [oo], pre, w_in, w_down, 3, d_pre)
        s, u = send(add(t3[:half], s), add(t3[half:], u))
        x_otb, x_obb = send(x_lot[:, m:], x_rob[:, m:])
        dw_down = grad_w_down(pre, [lo, ro, own, oo], [dy_lo, dy_ro, dy, dy_ot, dy_ob])
        dw_in = grad_w_in([x_lot, x_lob, x_rot, x_rob, x, x_ota, x_oba], d_pre, 0, d)
        s, u = send(add(rest_a, s), add(rest_b, u))
        dw_in = grad_w_in([x_lot, x_lob, x_rot, x_rob, x, x_otb, x_obb], d_pre, 1, d, dw_in)
        dx = jnp.concatenate([add(t0[:half], s), add(t0[half:], u)])
        return dx, dw_in, dw_down

    tokens = P(("dp", "tp"), None)
    return jax.shard_map(
        step,
        mesh=mesh,
        in_specs=(tokens, tokens, P("dp", "tp"), P(None, "tp"), P("tp", None)),
        out_specs=(tokens, P("dp", "tp"), tokens),
        check_vma=False,
    )
```

time: 267 us -> 271 us (1.015)
  Pallas kernels: 0 us -> 142 us
  matrix products: 110 us -> 0 us
  waiting for transfers between devices: 122 us -> 76.9 us
  starting transfers between devices: 0.18 us -> 26.4 us
  other arithmetic: 0 us -> 13.7 us
  between operations: 13.8 us -> 0.8 us
  local copies, waits for them, and re-layouts: 21.4 us -> 10.5 us
    pallas_call x0 -> x6, Pallas kernels: none -> 142 us  [the longest x3 71.2 us: backward(): pl.pallas_call(functools.partial(backward_body, nd, len(dys), blocks, len...]
    dot_general x4 -> x0, matrix products: 110 us -> none  [the longest x2 57.1 us: by_group(): jnp.einsum('gta,gtb->gab', a, b, preferred_element_type=jnp.float32)]
    unnamed x5 -> x0, waiting for transfers between devices: 93.3 us -> none
    ppermute x0 -> x18, waiting for transfers between devices: none -> 76.9 us  [the longest x9 66.3 us: send(): a = lax.ppermute(a, 'tp', right)]
    reshape x1 -> x0, waiting for transfers between devices: 28.7 us -> none  [by_group(): a, b = (t.reshape(groups, -1, t.shape[-1]) for t in (a, b))]
    ppermute x0 -> x18, starting transfers between devices: none -> 26.4 us  [the longest x9 19.3 us: send(): b = lax.ppermute(b, 'tp', left)]
    unnamed x3 -> x14, local copies, waits for them, and re-layouts: 21.4 us -> 0.84 us
    convert_element_type x0 -> x4, other arithmetic: none -> 11 us  [add(): return (term + got.astype(F32)).astype(BF16)]
  transfers between devices with their start and end apart: 3 -> 18, of which waited for: 3 -> 4; matrix products, arithmetic and copies ran while one was open for 48% -> 7% of each run, Pallas kernels for 0% -> 53%
where the time goes in v1:
time: 271 us; the launch traced here: 270 us
  Pallas kernels  142 us (52%)
  waiting for transfers between devices  76.9 us (28%)
  starting transfers between devices  26.4 us (10%)
  other arithmetic  13.7 us (5%)
  local copies, waits for them, and re-layouts  10.5 us (4%)
    pallas_call x3, Pallas kernels, backward(): pl.pallas_call(functools.partial(backward_body, nd, len(dys), blocks, len...  71.2 us
    ppermute x9, waiting for transfers between devices, send(): a = lax.ppermute(a, 'tp', right)  66.3 us
    pallas_call x2, Pallas kernels, grad_w_in(): pl.pallas_call(functools.partial(dw_in_body, columns), grid=(ff // tn,),...  40.4 us
    pallas_call x1, Pallas kernels, grad_w_down(): pl.pallas_call(functools.partial(dw_down_body, len(dys)), grid_spec=pltpu...  30.6 us
    ppermute x9, starting transfers between devices, send(): b = lax.ppermute(b, 'tp', left)  19.3 us
    convert_element_type x4, other arithmetic, add(): return (term + got.astype(F32)).astype(BF16)  11 us
    ppermute x9, waiting for transfers between devices, send(): b = lax.ppermute(b, 'tp', left)  10.6 us
    ppermute x9, starting transfers between devices, send(): a = lax.ppermute(a, 'tp', right)  7.07 us
  transfers between devices with their start and end apart: 18, of which 4 were waited for; matrix products, arithmetic and copies ran while one was open for 7% of the time, Pallas kernels for 53%

profile of v1, /device:TPU:112, one launch (start us, length us, event | category | flops | bytes accessed | tf_op | source)
XLA Modules:
  0.0 270.4 jit_solution(9089602727426555724)
XLA Ops:
  0.6 2.4 collective-permute-start
  3.1 1.6 collective-permute-start.1
  4.7 3.1 %fusion = (bf16[176,3072]{1,0:T(8,128)(2,1)}, bf16[176,3072]{1,0:T(8,128)(2,1)}) fusion(bf16[352,3072]{1,0:T(8,128)(2,1)} %refs_4_.10), kind=kLoop, calls=%fused_computation.9 | loop fusion | bytes 4325376 | tf_op jit(solution)/shard_map/slice | solution.py:195
  7.8 0.4 collective-permute-start.11
  8.1 2.9 %collective-permute-start.13 = (bf16[176,3072]{1,0:T(8,128)(2,1)}, bf16[176,3072]{1,0:T(8,128)(2,1)S(1)}, u32[]{:S(2)}, u32[]{:S(2)}) collective-permute-start(bf16[176,3072]{1,0:T(8,128)(2,1)} %get-tuple-element.25), channel_id=1, source_target_pairs={{0,3},{1,0},{2,1},{3,2},{4,7},{5,4},{6,5},{7,6},{8,11},{9,8},{10,9... | collective-permute-start | bytes 3244040 | tf_op jit(solution)/shard_map/ppermute | solution.py:182
  11.0 0.0 collective-permute-start.10
  11.0 0.7 pad_add_fusion.refs_0_
  11.7 0.6 pad_add_fusion.1.refs_0_
  12.3 20.8 %shard_map.76 = (bf16[1408,2304]{1,0:T(8,128)(2,1)}, f32[352,3072]{1,0:T(8,128)}) custom-call(s32[1]{0:T(128)} %bitcast.refs_0_, bf16[352,3072]{1,0:T(8,128)(2,1)} %refs_7_.3, bf16[1408,2304]{1,0:T(8,128)(2,1)} %refs_4_.11, bf16[2304,3072]{1,0:T(8,128)(2,1)} %refs_5_.3, bf16[3072,2304]{1,0:T(8,128)(2,1)} %refs_6_.3), custom_call_target="tpu_custom_call" | custom-call | flops 9965666304 | bytes 28311552 | tf_op jit(solution)/shard_map/pallas_call | solution.py:78
  33.0 65.2 %collective-permute-done.10.refs_0_ = bf16[176,3072]{1,0:T(8,128)(2,1)S(1)} collective-permute-done((bf16[176,3072]{1,0:T(8,128)(2,1)}, bf16[176,3072]{1,0:T(8,128)(2,1)S(1)}, u32[]{:S(2)}, u32[]{:S(2)}) %collective-permute-start.10) | collective-permute-done | bytes 1081376 | tf_op jit(solution)/shard_map/ppermute | solution.py:181
  98.3 1.0 fusion.2
  99.2 0.0 collective-permute-done.refs_2_.refs_5_
  99.2 2.3 slice.48
  101.5 0.2 collective-permute-start.2
  101.7 2.3 slice.49
  104.0 3.1 %collective-permute-start.3 = (bf16[176,3072]{1,0:T(8,128)(2,1)}, bf16[176,3072]{1,0:T(8,128)(2,1)}, u32[]{:S(2)}, u32[]{:S(2)}) collective-permute-start(bf16[176,3072]{1,0:T(8,128)(2,1)} %slice.49), channel_id=1, source_target_pairs={{0,3},{1,0},{2,1},{3,2},{4,7},{5,4},{6,5},{7,6},{8,11},{9,8},{10,9... | collective-permute-start | bytes 3244040 | tf_op jit(solution)/shard_map/ppermute | solution.py:182
  107.1 29.7 %shard_map.77 = (bf16[1408,2304]{1,0:T(8,128)(2,1)}, bf16[176,3072]{1,0:T(8,128)(2,1)}, bf16[176,3072]{1,0:T(8,128)(2,1)}, f32[176,3072]{1,0:T(8,128)}, f32[176,3072]{1,0:T(8,128)}) custom-call(s32[2]{0:T(128)} %pad_add_fusion.refs_0_, bf16[1408,2304]{1,0:T(8,128)(2,1)} %get-tuple-element.13.refs_1_, ...), custom_call_target="tpu_custom_call", output_to_operand_aliasing={{0}: (1, {})} | custom-call | flops 19931332608 | bytes 28311552 | tf_op jit(solution)/shard_map/pallas_call | solution.py:78
  136.8 0.0 collective-permute-start.4
  136.8 0.0 collective-permute-done.13.refs_3_
  136.9 3.2 %collective-permute-start.7 = (bf16[176,3072]{1,0:T(8,128)(2,1)}, bf16[176,3072]{1,0:T(8,128)(2,1)S(1)}, u32[]{:S(2)}, u32[]{:S(2)}) collective-permute-start(bf16[176,3072]{1,0:T(8,128)(2,1)} %get-tuple-element.19), channel_id=1, source_target_pairs={{0,3},{1,0},{2,1},{3,2},{4,7},{5,4},{6,5},{7,6},{8,11},{9,8},{10,9... | collective-permute-start | bytes 3244040 | tf_op jit(solution)/shard_map/ppermute | solution.py:182
  140.1 1.1 fusion.1
  141.1 0.0 collective-permute-done.2.refs_2_.refs_8_
  141.1 0.1 collective-permute-start.12
  141.2 0.0 collective-permute-done.3.refs_3_.refs_9_
  141.2 2.0 collective-permute-start.14
  143.2 20.7 %shard_map.78 = (bf16[1408,2304]{1,0:T(8,128)(2,1)}, f32[352,3072]{1,0:T(8,128)}) custom-call(s32[1]{0:T(128)} %bitcast.3.refs_0_, bf16[1408,2304]{1,0:T(8,128)(2,1)} %get-tuple-element.15.refs_1_, bf16[176,3072]{1,0:T(8,128)(2,1)} %collective-permute-done.2.refs_2_.refs_8_, ...), custom_call_target="tpu_custom_call", output_to_operand_aliasing={{0}: (1, {})} | custom-call | flops 9965666304 | bytes 28311552 | tf_op jit(solution)/shard_map/pallas_call | solution.py:78
  163.9 1.1 collective-permute-done.4
  165.0 0.0 collective-permute-done.7
  165.0 4.0 %add_convert_fusion.5 = (bf16[176,3072]{1,0:T(8,128)(2,1)}, bf16[176,3072]{1,0:T(8,128)(2,1)S(1)}) fusion(bf16[176,3072]{1,0:T(8,128)(2,1)S(1)} %collective-permute-done.4, f32[352,3072]{1,0:T(8,128)} %get-tuple-element.16, bf16[176,3072]{1,0:T(8,128)(2,1)S(1)} %collective-permute-done.7), kind=kLoop, calls=%fused_computation.6 | loop fusion | flops 3244032 | bytes 8650752 | tf_op jit(solution)/shard_map/convert_element_type | solution.py:186
  168.9 3.2 %collective-permute-start.8 = (bf16[176,3072]{1,0:T(8,128)(2,1)S(1)}, bf16[176,3072]{1,0:T(8,128)(2,1)}, u32[]{:S(2)}, u32[]{:S(2)}) collective-permute-start(bf16[176,3072]{1,0:T(8,128)(2,1)S(1)} %get-tuple-element.24), channel_id=1, source_target_pairs={{0,3},{1,0},{2,1},{3,2},{4,7},{5,4},{6,5},{7,6},{8,11},{9,8},{10,9... | collective-permute-start | bytes 3244040 | tf_op jit(solution)/shard_map/ppermute | solution.py:182
  172.2 30.6 %shard_map.81 = bf16[2304,3072]{1,0:T(8,128)(2,1)} custom-call(s32[4]{0:T(128)} %pad_add_fusion.1.refs_0_, bf16[1408,2304]{1,0:T(8,128)(2,1)} %refs_4_.11, bf16[1408,2304]{1,0:T(8,128)(2,1)} %refs_4_.11, bf16[1408,2304]{1,0:T(8,128)(2,1)} %refs_4_.11, bf16[1408,2304]{1,0:T(8,128)(2,1)} %refs_4_.11, bf16[352,3072]{1,0:T(8,128)(2,1)} %collective-permute-done.refs_2_.refs_5_, ...), custom_call_target="tpu_custom_call" | custom-call | flops 19931332608 | bytes 37945344 | tf_op jit(solution)/shard_map/pallas_call | solution.py:120
  202.8 0.0 collective-permute-done.5
  202.8 0.1 collective-permute-start.16
  202.9 0.0 copy-start.2
  202.9 2.6 add_convert_fusion.4
  205.5 2.9 %collective-permute-done.8 = bf16[176,3072]{1,0:T(8,128)(2,1)} collective-permute-done((bf16[176,3072]{1,0:T(8,128)(2,1)S(1)}, bf16[176,3072]{1,0:T(8,128)(2,1)}, u32[]{:S(2)}, u32[]{:S(2)}) %collective-permute-start.8) | collective-permute-done | bytes 1081376 | tf_op jit(solution)/shard_map/ppermute | solution.py:182
  208.4 3.8 %collective-permute-start.17 = (bf16[176,1536]{1,0:T(8,128)(2,1)S(1)}, bf16[176,1536]{1,0:T(8,128)(2,1)S(1)}, u32[]{:S(2)}, u32[]{:S(2)}) collective-permute-start(bf16[176,1536]{1,0:T(8,128)(2,1)S(1)} %copy-done.4), channel_id=1, source_target_pairs={{0,3},{1,0},{2,1},{3,2},{4,7},{5,4},{6,5},{7,6},{8,11},{9,8},{10,9... | collective-permute-start | bytes 1622024 | tf_op jit(solution)/shard_map/ppermute | solution.py:182
  212.2 1.5 add_convert_fusion.1
  213.7 0.0 collective-permute-done.11.refs_1_
  213.7 0.1 collective-permute-start.15
  213.9 2.0 collective-permute-start.6
  215.9 1.3 collective-permute-start.9
  217.2 7.7 %collective-permute-done.17.refs_6_ = bf16[176,1536]{1,0:T(8,128)(2,1)S(1)} collective-permute-done((bf16[176,1536]{1,0:T(8,128)(2,1)S(1)}, bf16[176,1536]{1,0:T(8,128)(2,1)S(1)}, u32[]{:S(2)}, u32[]{:S(2)}) %collective-permute-start.17) | collective-permute-done | bytes 540704 | tf_op jit(solution)/shard_map/ppermute | solution.py:182
  224.9 0.8 copy-done.6
  225.7 20.2 %shard_map.79.refs_8_ = bf16[3072,2304]{1,0:T(8,128)(2,1)} custom-call(bf16[176,3072]{1,0:T(8,128)(2,1)} %copy-done.1, bf16[176,3072]{1,0:T(8,128)(2,1)} %collective-permute-done.11.refs_1_, bf16[176,3072]{1,0:T(8,128)(2,1)} %collective-permute-done.12.refs_2_, bf16[176,3072]{1,0:T(8,128)(2,1)} %copy-done, bf16[352,3072]{1,0:T(8,128)(2,1)} %refs_4_.10, ...), custom_call_target="tpu_custom_call" | custom-call | flops 9965666304 | bytes 17891328 | tf_op jit(solution)/shard_map/pallas_call | solution.py:160
  245.9 20.2 %shard_map.80 = bf16[3072,2304]{1,0:T(8,128)(2,1)} custom-call(bf16[176,3072]{1,0:T(8,128)(2,1)} %copy-done.1, bf16[176,3072]{1,0:T(8,128)(2,1)} %collective-permute-done.11.refs_1_, bf16[176,3072]{1,0:T(8,128)(2,1)} %collective-permute-done.12.refs_2_, bf16[176,3072]{1,0:T(8,128)(2,1)} %copy-done, ...), custom_call_target="tpu_custom_call", output_to_operand_aliasing={{}: (8, {})} | custom-call | flops 9965666304 | bytes 17891328 | tf_op jit(solution)/shard_map/pallas_call | solution.py:160
  266.1 2.9 %add_convert_fusion.3 = (bf16[176,3072]{1,0:T(8,128)(2,1)S(1)}, bf16[176,3072]{1,0:T(8,128)(2,1)S(1)}) fusion(bf16[176,3072]{1,0:T(8,128)(2,1)S(1)} %collective-permute-done.6, f32[352,3072]{1,0:T(8,128)} %get-tuple-element.12, bf16[176,3072]{1,0:T(8,128)(2,1)S(1)} %collective-permute-done.9), kind=kLoop, calls=%fused_computation.4 | loop fusion | flops 3244032 | bytes 8650752 | tf_op jit(solution)/shard_map/convert_element_type | solution.py:186
  269.0 1.5 pad_maximum_fusion
  (20 shorter events, 0.0 us)
Async XLA Ops:
  0.6 98.6 %collective-permute-start = (bf16[352,3072]{1,0:T(8,128)(2,1)}, bf16[352,3072]{1,0:T(8,128)(2,1)}, u32[]{:S(2)}, u32[]{:S(2)}) collective-permute-start(bf16[352,3072]{1,0:T(8,128)(2,1)} %refs_7_.3), channel_id=1, source_target_pairs={{0,1},{1,2},{2,3},{3,0},{4,5},{5,6},{6,7},{7,4},{8,9},{9,10},{10,1... | collective-permute-start | bytes 6488072 | tf_op jit(solution)/shard_map/ppermute | solution.py:181
  3.1 98.7 %collective-permute-start.1 = (bf16[352,3072]{1,0:T(8,128)(2,1)}, bf16[352,3072]{1,0:T(8,128)(2,1)}, u32[]{:S(2)}, u32[]{:S(2)}) collective-permute-start(bf16[352,3072]{1,0:T(8,128)(2,1)} %refs_7_.3), channel_id=1, source_target_pairs={{0,3},{1,0},{2,1},{3,2},{4,7},{5,4},{6,5},{7,6},{8,11},{9,8},{10,9... | collective-permute-start | bytes 6488072 | tf_op jit(solution)/shard_map/ppermute | solution.py:182
  7.8 206.0 %collective-permute-start.11 = (bf16[176,3072]{1,0:T(8,128)(2,1)}, bf16[176,3072]{1,0:T(8,128)(2,1)}, u32[]{:S(2)}, u32[]{:S(2)}) collective-permute-start(bf16[176,3072]{1,0:T(8,128)(2,1)} %get-tuple-element.25), channel_id=1, source_target_pairs={{0,1},{1,2},{2,3},{3,0},{4,5},{5,6},{6,7},{7,4},{8,9},{9,10},{10,1... | collective-permute-start | bytes 3244040 | tf_op jit(solution)/shard_map/ppermute | solution.py:181
  8.1 128.7 %collective-permute-start.13 = (bf16[176,3072]{1,0:T(8,128)(2,1)}, bf16[176,3072]{1,0:T(8,128)(2,1)S(1)}, u32[]{:S(2)}, u32[]{:S(2)}) collective-permute-start(bf16[176,3072]{1,0:T(8,128)(2,1)} %get-tuple-element.25), channel_id=1, source_target_pairs={{0,3},{1,0},{2,1},{3,2},{4,7},{5,4},{6,5},{7,6},{8,11},{9,8},{10,9... | collective-permute-start | bytes 3244040 | tf_op jit(solution)/shard_map/ppermute | solution.py:182
  11.0 87.3 %collective-permute-start.10 = (bf16[176,3072]{1,0:T(8,128)(2,1)}, bf16[176,3072]{1,0:T(8,128)(2,1)S(1)}, u32[]{:S(2)}, u32[]{:S(2)}) collective-permute-start(bf16[176,3072]{1,0:T(8,128)(2,1)} %get-tuple-element.26), channel_id=1, source_target_pairs={{0,1},{1,2},{2,3},{3,0},{4,5},{5,6},{6,7},{7,4},{8,9},{9,10},{10,1... | collective-permute-start | bytes 3244040 | tf_op jit(solution)/shard_map/ppermute | solution.py:181
  98.3 3.3 %copy-start.1 = (bf16[176,3072]{1,0:T(8,128)(2,1)}, bf16[176,3072]{1,0:T(8,128)(2,1)S(1)}, u32[]{:S(2)}) copy-start(bf16[176,3072]{1,0:T(8,128)(2,1)S(1)} %collective-permute-done.10.refs_0_) | copy-start | bytes 3244036
  101.5 39.6 %collective-permute-start.2 = (bf16[176,3072]{1,0:T(8,128)(2,1)}, bf16[176,3072]{1,0:T(8,128)(2,1)}, u32[]{:S(2)}, u32[]{:S(2)}) collective-permute-start(bf16[176,3072]{1,0:T(8,128)(2,1)} %slice.48), channel_id=1, source_target_pairs={{0,1},{1,2},{2,3},{3,0},{4,5},{5,6},{6,7},{7,4},{8,9},{9,10},{10,1... | collective-permute-start | bytes 3244040 | tf_op jit(solution)/shard_map/ppermute | solution.py:181
  104.0 37.2 %collective-permute-start.3 = (bf16[176,3072]{1,0:T(8,128)(2,1)}, bf16[176,3072]{1,0:T(8,128)(2,1)}, u32[]{:S(2)}, u32[]{:S(2)}) collective-permute-start(bf16[176,3072]{1,0:T(8,128)(2,1)} %slice.49), channel_id=1, source_target_pairs={{0,3},{1,0},{2,1},{3,2},{4,7},{5,4},{6,5},{7,6},{8,11},{9,8},{10,9... | collective-permute-start | bytes 3244040 | tf_op jit(solution)/shard_map/ppermute | solution.py:182
  136.8 28.2 %collective-permute-start.4 = (bf16[176,3072]{1,0:T(8,128)(2,1)}, bf16[176,3072]{1,0:T(8,128)(2,1)S(1)}, u32[]{:S(2)}, u32[]{:S(2)}) collective-permute-start(bf16[176,3072]{1,0:T(8,128)(2,1)} %get-tuple-element.17), channel_id=1, source_target_pairs={{0,1},{1,2},{2,3},{3,0},{4,5},{5,6},{6,7},{7,4},{8,9},{9,10},{10,1... | collective-permute-start | bytes 3244040 | tf_op jit(solution)/shard_map/ppermute | solution.py:181
  136.8 27.1 %copy-start = (bf16[176,3072]{1,0:T(8,128)(2,1)}, bf16[176,3072]{1,0:T(8,128)(2,1)S(1)}, u32[]{:S(2)}) copy-start(bf16[176,3072]{1,0:T(8,128)(2,1)S(1)} %collective-permute-done.13.refs_3_) | copy-start | bytes 3244036
  136.9 28.1 %collective-permute-start.7 = (bf16[176,3072]{1,0:T(8,128)(2,1)}, bf16[176,3072]{1,0:T(8,128)(2,1)S(1)}, u32[]{:S(2)}, u32[]{:S(2)}) collective-permute-start(bf16[176,3072]{1,0:T(8,128)(2,1)} %get-tuple-element.19), channel_id=1, source_target_pairs={{0,3},{1,0},{2,1},{3,2},{4,7},{5,4},{6,5},{7,6},{8,11},{9,8},{10,9... | collective-permute-start | bytes 3244040 | tf_op jit(solution)/shard_map/ppermute | solution.py:182
  141.1 72.7 %collective-permute-start.12 = (bf16[176,3072]{1,0:T(8,128)(2,1)}, bf16[176,3072]{1,0:T(8,128)(2,1)}, u32[]{:S(2)}, u32[]{:S(2)}) collective-permute-start(bf16[176,3072]{1,0:T(8,128)(2,1)} %get-tuple-element.26), channel_id=1, source_target_pairs={{0,3},{1,0},{2,1},{3,2},{4,7},{5,4},{6,5},{7,6},{8,11},{9,8},{10,9... | collective-permute-start | bytes 3244040 | tf_op jit(solution)/shard_map/ppermute | solution.py:182
  141.2 104.6 %collective-permute-start.14 = (bf16[176,1536]{1,0:T(8,128)(2,1)S(1)}, bf16[176,1536]{1,0:T(8,128)(2,1)}, u32[]{:S(2)}, u32[]{:S(2)}) collective-permute-start(bf16[176,1536]{1,0:T(8,128)(2,1)S(1)} %get-tuple-element.30), channel_id=1, source_target_pairs={{0,1},{1,2},{2,3},{3,0},{4,5},{5,6},{6,7},{7,4},{8,9},{9,10},{10,1... | collective-permute-start | bytes 1622024 | tf_op jit(solution)/shard_map/ppermute | solution.py:181
  168.9 33.8 %collective-permute-start.5 = (bf16[176,3072]{1,0:T(8,128)(2,1)}, bf16[176,3072]{1,0:T(8,128)(2,1)}, u32[]{:S(2)}, u32[]{:S(2)}) collective-permute-start(bf16[176,3072]{1,0:T(8,128)(2,1)} %get-tuple-element.23), channel_id=1, source_target_pairs={{0,1},{1,2},{2,3},{3,0},{4,5},{5,6},{6,7},{7,4},{8,9},{9,10},{10,1... | collective-permute-start | bytes 3244040 | tf_op jit(solution)/shard_map/ppermute | solution.py:181
  168.9 33.9 %copy-start.3 = (f32[176,3072]{1,0:T(8,128)S(1)}, f32[176,3072]{1,0:T(8,128)}, u32[]{:S(2)}) copy-start(f32[176,3072]{1,0:T(8,128)} %get-tuple-element.14) | copy-start | bytes 6488068
  168.9 39.4 %collective-permute-start.8 = (bf16[176,3072]{1,0:T(8,128)(2,1)S(1)}, bf16[176,3072]{1,0:T(8,128)(2,1)}, u32[]{:S(2)}, u32[]{:S(2)}) collective-permute-start(bf16[176,3072]{1,0:T(8,128)(2,1)S(1)} %get-tuple-element.24), channel_id=1, source_target_pairs={{0,3},{1,0},{2,1},{3,2},{4,7},{5,4},{6,5},{7,6},{8,11},{9,8},{10,9... | collective-permute-start | bytes 3244040 | tf_op jit(solution)/shard_map/ppermute | solution.py:182
  202.8 13.1 %collective-permute-start.16 = (bf16[176,1536]{1,0:T(8,128)(2,1)}, bf16[176,1536]{1,0:T(8,128)(2,1)S(1)}, u32[]{:S(2)}, u32[]{:S(2)}) collective-permute-start(bf16[176,1536]{1,0:T(8,128)(2,1)} %get-tuple-element.29), channel_id=1, source_target_pairs={{0,1},{1,2},{2,3},{3,0},{4,5},{5,6},{6,7},{7,4},{8,9},{9,10},{10,1... | collective-permute-start | bytes 1622024 | tf_op jit(solution)/shard_map/ppermute | solution.py:181
  202.9 5.5 %copy-start.4 = (bf16[176,1536]{1,0:T(8,128)(2,1)S(1)}, bf16[176,1536]{1,0:T(8,128)(2,1)}, u32[]{:S(2)}) copy-start(bf16[176,1536]{1,0:T(8,128)(2,1)} %get-tuple-element.27) | copy-start | bytes 1622020
  202.9 9.3 %copy-start.2 = (f32[176,3072]{1,0:T(8,128)S(1)}, f32[176,3072]{1,0:T(8,128)}, u32[]{:S(2)}) copy-start(f32[176,3072]{1,0:T(8,128)} %get-tuple-element.18) | copy-start | bytes 6488068
  208.4 16.5 %collective-permute-start.17 = (bf16[176,1536]{1,0:T(8,128)(2,1)S(1)}, bf16[176,1536]{1,0:T(8,128)(2,1)S(1)}, u32[]{:S(2)}, u32[]{:S(2)}) collective-permute-start(bf16[176,1536]{1,0:T(8,128)(2,1)S(1)} %copy-done.4), channel_id=1, source_target_pairs={{0,3},{1,0},{2,1},{3,2},{4,7},{5,4},{6,5},{7,6},{8,11},{9,8},{10,9... | collective-permute-start | bytes 1622024 | tf_op jit(solution)/shard_map/ppermute | solution.py:182
  213.7 32.1 %collective-permute-start.15 = (bf16[176,1536]{1,0:T(8,128)(2,1)}, bf16[176,1536]{1,0:T(8,128)(2,1)}, u32[]{:S(2)}, u32[]{:S(2)}) collective-permute-start(bf16[176,1536]{1,0:T(8,128)(2,1)} %get-tuple-element.28), channel_id=1, source_target_pairs={{0,3},{1,0},{2,1},{3,2},{4,7},{5,4},{6,5},{7,6},{8,11},{9,8},{10,9... | collective-permute-start | bytes 1622024 | tf_op jit(solution)/shard_map/ppermute | solution.py:182
  213.9 52.2 %collective-permute-start.6 = (bf16[176,3072]{1,0:T(8,128)(2,1)}, bf16[176,3072]{1,0:T(8,128)(2,1)S(1)}, u32[]{:S(2)}, u32[]{:S(2)}) collective-permute-start(bf16[176,3072]{1,0:T(8,128)(2,1)} %add_convert_fusion.4), channel_id=1, source_target_pairs={{0,1},{1,2},{2,3},{3,0},{4,5},{5,6},{6,7},{7,4},{8,9},{9,10},{10,1... | collective-permute-start | bytes 3244040 | tf_op jit(solution)/shard_map/ppermute | solution.py:181
  215.8 9.0 %copy-start.5 = (bf16[176,1536]{1,0:T(8,128)(2,1)}, bf16[176,1536]{1,0:T(8,128)(2,1)S(1)}, u32[]{:S(2)}) copy-start(bf16[176,1536]{1,0:T(8,128)(2,1)S(1)} %collective-permute-done.16.refs_5_) | copy-start | bytes 1622020
  215.9 50.2 %collective-permute-start.9 = (bf16[176,3072]{1,0:T(8,128)(2,1)S(1)}, bf16[176,3072]{1,0:T(8,128)(2,1)S(1)}, u32[]{:S(2)}, u32[]{:S(2)}) collective-permute-start(bf16[176,3072]{1,0:T(8,128)(2,1)S(1)} %add_convert_fusion.1), channel_id=1, source_target_pairs={{0,3},{1,0},{2,1},{3,2},{4,7},{5,4},{6,5},{7,6},{8,11},{9,8},{10,9... | collective-permute-start | bytes 3244040 | tf_op jit(solution)/shard_map/ppermute | solution.py:182
  224.9 0.8 copy-start.6
